TPU v7x, 256 devices: a 8x8x2 block of a 8x8x16 slice. The times are simulated.
256 devices in a mesh: grp: 2 (over z), row: 16 (over x, core), col: 8 (over y).
Axes of the slice: x: 8, y: 8, z: 2, core: 2. Of those that a mesh axis runs over, the one named last changes fastest.
The devices are a block of a 8x8x16 slice.
Arguments:
- perturbation: bfloat16 [4, 12000, 12000], P('grp', 'row', 'col'), parts along dimension 0, may hold values from -96 to 96
- occ_coeffs: bfloat16 [12000, 2000], P('row', 'col'), may hold values from -0.0546875 to 0.0546875
- vir_coeffs: bfloat16 [12000, 512], P('col', 'row'), may hold values from -0.0546875 to 0.0546875
- occ_energies: float32 [2000], replicated, may hold values from -1 to -0.1
- vir_energies: float32 [512], replicated, may hold values from 0.1 to 1.5
Outputs:
- density_response: bfloat16 [4, 12000, 12000], P('grp', 'row', 'col'), parts along dimension 0
There are 2 independent parts, one for each index of `grp`. A program takes and returns all parts, laid end to end along the dimension named above; an argument that names none is the same for every part. Nothing has to cross between parts.
All inputs are finite; a program needn't handle non-finite values.
Results may differ from a plain program's by a relative error of at most 0.0098.
Values may be sent and summed in bfloat16 or wider, within the bound.
No kernel may reach another device: no remote copies, remote signals or barrier semaphores. Data moves between devices by JAX's collectives and lax.ppermute only.
A program may use at most 64 MiB of HBM per device.

v0:
```python
import jax
import jax.numpy as jnp
from jax import lax
from jax.sharding import Mesh
from jax.sharding import PartitionSpec as P

ROW = ("row_0", "row_1")


def joined_along(pieces, dim):
    pieces = jnp.moveaxis(pieces, 0, dim)
    dims = pieces.shape
    return pieces.reshape(*dims[:dim], dims[dim] * dims[dim + 1], *dims[dim + 2 :])


def sent_to_all(shard, axis):
    copies = jnp.broadcast_to(shard, (lax.axis_size(axis), *shard.shape))
    return lax.all_to_all(copies, axis, split_axis=0, concat_axis=0, tiled=True)


def collect(shard, axis, dim):
    return joined_along(sent_to_all(shard, axis), dim)


def cut_along(shard, dim, count):
    before, after = (shard.shape[:dim], shard.shape[dim + 1 :])
    return jnp.moveaxis(shard.reshape(*before, count, -1, *after), dim, 0)


def summed_on_arrival(shard, axis, dim):
    count = lax.axis_size(axis)
    pieces = lax.all_to_all(cut_along(shard, dim, count), axis, 0, 0, tiled=True)
    return jnp.sum(pieces.astype(jnp.float32), axis=0)


def padded_to(lines, count):
    spare = -len(lines) % count
    return jnp.pad(lines, [(0, spare)] + [(0, 0)] * (lines.ndim - 1))


def reduced_to_own(pieces, axes, order):
    inside = pieces.shape[1:]
    pieces = pieces.reshape(*(lax.axis_size(a) for a in axes), *inside)
    pieces = jnp.moveaxis(pieces, order, range(len(axes))).reshape(-1, *inside)
    for k in order:
        pieces = lax.psum_scatter(pieces, axes[k], scatter_dimension=0, tiled=True)
    return pieces[0]


def stacked_from(shard, axes, order):
    pieces = shard[None]
    for k in order:
        pieces = lax.all_gather(pieces, axes[k], axis=0, tiled=True)
    carried = [lax.axis_size(axes[k]) for k in reversed(order)]
    pieces = pieces.reshape(*carried, *shard.shape)
    turned = sorted(range(len(order)), key=lambda place: order[len(order) - 1 - place])
    return pieces.transpose(*turned, *range(len(order), pieces.ndim)).reshape(-1, *shard.shape)


def sum_by_parts(shard, axes, order):
    count, lines = (lax.axis_size(axes), shard.reshape(-1, *shard.shape[1:][-1:]))
    pieces = padded_to(lines, count).reshape(count, -1, *lines.shape[1:])
    own = reduced_to_own(pieces, axes, order)
    whole = stacked_from(own, axes, order[::-1]).reshape(-1, *lines.shape[1:])
    return whole[: len(lines)].reshape(shard.shape)


def per_device(perturbation, occ_coeffs, vir_coeffs, occ_energies, vir_energies):
    occ_rows = lax.all_gather(occ_coeffs, "col", axis=1, tiled=True)
    vir_rows = collect(vir_coeffs, ROW, 1)
    share = vir_rows.shape[1] // lax.axis_size("col")
    image = summed_on_arrival(
        jnp.einsum(
            "pij,jv->vpi", perturbation, vir_rows, preferred_element_type=jnp.float32
        ).astype(jnp.bfloat16),
        "col",
        0,
    )
    partial_value = jnp.einsum(
        "io,vpi->pov", occ_rows.astype(jnp.float32), image, precision=lax.Precision.HIGHEST
    )
    coupling = sum_by_parts(partial_value, ROW, (0, 1))
    offset = lax.axis_index("col") * share
    energies = lax.dynamic_slice_in_dim(vir_energies, offset, share, 0)
    gaps = occ_energies[:, None] - energies[None, :]
    response = (coupling / gaps[None, :, :]).astype(jnp.bfloat16)
    mixed = jnp.einsum(
        "io,pov->piv", occ_rows, response, preferred_element_type=jnp.float32
    ).astype(jnp.bfloat16)
    total = jnp.einsum(
        "piv,jv->pij", collect(mixed, "col", 2), vir_rows, preferred_element_type=jnp.float32
    )
    return total.astype(jnp.bfloat16)


def solution(mesh):
    torus = Mesh(
        mesh.devices.reshape(mesh.shape["grp"], 8, 2, mesh.shape["col"]),
        ("grp", "row_0", "row_1", "col"),
    )
    in_specs = (P("grp", ROW, "col"), P(ROW, "col"), P("col", ROW), P(), P())
    out_specs = P("grp", ROW, "col")
    return jax.shard_map(
        per_device, mesh=torus, in_specs=in_specs, out_specs=out_specs, check_vma=False
    )
```

profile of v0, /device:TPU:516, one launch (start us, length us, event | category | flops | bytes accessed | tf_op | source)
XLA Modules:
  0.0 288.0 jit_solution(6391762949328565553)
XLA Ops:
  6.5 2.2 broadcast_in_dim.4
  8.7 22.8 %all-to-all-start = ((bf16[16,1500,32]{1,2,0:T(8,128)(2,1)}), bf16[16,1500,32]{1,2,0:T(8,128)(2,1)S(1)}, u32[]{:S(2)}, u32[]{:S(2)}) async-start(bf16[16,1500,32]{1,2,0:T(8,128)(2,1)} %broadcast_in_dim.4), calls=%async_computation | async-start | bytes 3145728 | tf_op jit(solution)/shard_map/all_to_all | solution.py:18
  31.5 0.1 all-gather.3.cloned.1.call-start
  31.6 0.7 all-gather.3.cloned.1.call-update
  32.3 35.1 %all-to-all-done = bf16[16,1500,32]{1,2,0:T(8,128)(2,1)S(1)} async-done(((bf16[16,1500,32]{1,2,0:T(8,128)(2,1)}), bf16[16,1500,32]{1,2,0:T(8,128)(2,1)S(1)}, u32[]{:S(2)}, u32[]{:S(2)}) %all-to-all-start) | async-done | bytes 1536032 | tf_op jit(solution)/shard_map/all_to_all | solution.py:18
  67.4 0.0 copy-start
  67.4 1.1 copy-done
  68.6 4.9 %fusion.9 = bf16[512,2,750]{0,2,1:T(8,128)(2,1)S(1)} fusion(bf16[1500,512,1]{0,1,2:T(8,128)(2,1)S(1)} %bitcast.40, bf16[2,750,1500]{2,0,1:T(2,128)(2,1)} %param.5), kind=kOutput, calls=%fused_computation.9 | convolution fusion | flops 2304768000 | bytes 7572000 | tf_op jit(solution)/shard_map/pij,jv->vpi/dot_general | solution.py:73
  73.5 0.7 copy.24
  74.2 1.3 copy.25
  75.5 4.5 %all-to-all-start.1 = ((bf16[8,64,2,750]{3,1,2,0:T(8,128)(2,1)}), bf16[8,64,2,750]{3,1,2,0:T(8,128)(2,1)}, u32[]{:S(2)}, u32[]{:S(2)}) async-start(bf16[8,64,2,750]{3,1,2,0:T(8,128)(2,1)} %copy.25), calls=%async_computation.1 | async-start | bytes 3145728 | tf_op jit(solution)/shard_map/all_to_all | solution.py:32
  80.0 0.1 reduce-scatter.3.cloned.1.call-start
  80.0 2.3 all-gather.3.cloned.1.call-done
  82.3 4.6 %copy.26 = bf16[8,250,750]{1,0,2:T(8,128)(2,1)} copy(bf16[8,250,750]{1,2,0:T(8,128)(2,1)} %all-gather.3.cloned.1.call-done) | data formatting | bytes 6000000 | tf_op jit(solution)/shard_map/all_gather | solution.py:69
  86.9 5.5 %reshape.42 = bf16[2000,750]{0,1:T(8,128)(2,1)S(1)} reshape(bf16[8,250,750]{1,0,2:T(8,128)(2,1)} %copy.26) | data formatting | bytes 6000000
  92.4 28.9 %all-to-all-done.1 = bf16[8,64,2,750]{3,1,2,0:T(8,128)(2,1)} async-done(((bf16[8,64,2,750]{3,1,2,0:T(8,128)(2,1)}), bf16[8,64,2,750]{3,1,2,0:T(8,128)(2,1)}, u32[]{:S(2)}, u32[]{:S(2)}) %all-to-all-start.1) | async-done | bytes 1536032 | tf_op jit(solution)/shard_map/all_to_all | solution.py:32
  121.3 1.7 convert_reduce_fusion
  123.0 1.5 fusion.6
  124.4 1.8 copy.28
  126.2 0.0 copy-start.2
  126.2 3.5 %reshape_reshape_reshape.3 = f32[16,250,64]{1,0,2:T(8,128)} reshape(f32[2,2000,64]{1,0,2:T(2,128)} %copy.28) | data formatting | bytes 2048000 | tf_op jit(solution)/shard_map/reshape;reshape;reshape | solution.py:44
  129.7 2.8 copy.29
  132.5 0.1 reduce-scatter.3.cloned.1.call-update
  132.6 0.1 reduce-scatter.5.cloned.1.call-start
  132.6 0.8 dynamic_slice.3
  133.4 36.3 %reduce-scatter.3.cloned.1.call-done = f32[2,250,64]{1,2,0:T(8,128)} async-done(((f32[16,250,64]{1,2,0:T(8,128)}), f32[2,250,64]{1,2,0:T(8,128)}) %reduce-scatter.3.cloned.1.call-update) | async-done | bytes 128016 | tf_op jit(solution)/shard_map/reduce_scatter | solution.py:46
  169.7 0.1 reduce-scatter.5.cloned.1.call-update
  169.7 0.0 copy-done.2
  169.7 0.9 broadcast_subtract_fusion
  170.7 16.2 %reduce-scatter.5.cloned.1.call-done = f32[1,250,64]{1,2,0:T(8,128)} async-done(((f32[2,250,64]{1,2,0:T(8,128)}), f32[1,250,64]{1,2,0:T(8,128)}) %reduce-scatter.5.cloned.1.call-update) | async-done | bytes 64016 | tf_op jit(solution)/shard_map/reduce_scatter | solution.py:46
  186.9 2.1 all_gather.10
  189.0 28.1 %all_gather.11 = f32[16,250,64]{1,2,0:T(8,128)S(1)} all-gather(f32[2,250,64]{1,2,0:T(8,128)S(1)} %all_gather.10), channel_id=1, replica_groups=mesh['grp'=2,'row_0'=8,'row_1'=2,'col'=8] {'row_0'}, dimensions={0}, use_global_device_ids=true | all-gather | bytes 1152000 | tf_op jit(solution)/shard_map/all_gather | solution.py:53
  217.1 1.6 copy.30
  218.7 3.7 %reshape_reshape_reshape_reshape.3 = f32[2,2000,64]{1,0,2:T(2,128)} reshape(f32[16,250,64]{1,0,2:T(8,128)} %copy.30) | data formatting | bytes 2048000 | tf_op jit(solution)/shard_map/reshape;reshape;reshape;reshape | solution.py:65
  222.4 1.9 divide_convert_fusion
  224.3 1.1 fusion.15
  225.4 0.1 broadcast_in_dim.10
  225.5 0.0 copy-start.1
  225.5 41.8 %all_to_all.15 = bf16[8,2,750,64]{2,3,1,0:T(8,128)(2,1)S(1)} all-to-all(bf16[8,2,750,64]{2,3,1,0:T(8,128)(2,1)S(1)} %broadcast_in_dim.10), channel_id=1, replica_groups=mesh['grp'=2,'row_0'=8,'row_1'=2,'col'=8] {'col'}, dimensions={0} | all-to-all | bytes 3072000 | tf_op jit(solution)/shard_map/all_to_all | solution.py:18
  267.4 0.1 copy.33
  267.5 0.0 copy-done.1
  267.5 4.7 %convolution_convert_fusion = bf16[2,750,1500]{2,1,0:T(8,128)(2,1)} fusion(bf16[2,750,512]{1,2,0:T(8,128)(2,1)S(1)} %bitcast.42, bf16[1500,512,1]{0,1,2:T(8,128)(2,1)S(1)} %bitcast.41), kind=kOutput, calls=%fused_computation.2 | convolution fusion | flops 2306249984 | bytes 7572000 | tf_op jit(solution)/shard_map/piv,jv->pij/dot_general | solution.py:90
  272.2 9.2 %copy.36 = bf16[2,750,1500]{2,0,1:T(2,128)(2,1)} copy(bf16[2,750,1500]{2,1,0:T(8,128)(2,1)} %convolution_convert_fusion) | data formatting | bytes 9000000 | tf_op jit(solution)/shard_map/convert_element_type | solution.py:93
Async XLA Ops:
  8.7 58.7 %all-to-all-start = ((bf16[16,1500,32]{1,2,0:T(8,128)(2,1)}), bf16[16,1500,32]{1,2,0:T(8,128)(2,1)S(1)}, u32[]{:S(2)}, u32[]{:S(2)}) async-start(bf16[16,1500,32]{1,2,0:T(8,128)(2,1)} %broadcast_in_dim.4), calls=%async_computation | async-start | bytes 3145728 | tf_op jit(solution)/shard_map/all_to_all | solution.py:18
  31.5 50.8 %all-gather.3.cloned.1.call-start = ((), (), s32[]{:S(2)}) async-start(), calls=%async_computation.7 | async-start | bytes 3465216 | tf_op jit(solution)/shard_map/all_gather | solution.py:69
  67.4 1.2 copy-start
  75.5 45.8 %all-to-all-start.1 = ((bf16[8,64,2,750]{3,1,2,0:T(8,128)(2,1)}), bf16[8,64,2,750]{3,1,2,0:T(8,128)(2,1)}, u32[]{:S(2)}, u32[]{:S(2)}) async-start(bf16[8,64,2,750]{3,1,2,0:T(8,128)(2,1)} %copy.25), calls=%async_computation.1 | async-start | bytes 3145728 | tf_op jit(solution)/shard_map/all_to_all | solution.py:32
  80.0 89.7 %reduce-scatter.3.cloned.1.call-start = ((), (), s32[]{:S(2)}) async-start(), calls=%async_computation.5 | async-start | bytes 1179648 | tf_op jit(solution)/shard_map/reduce_scatter | solution.py:46
  126.2 43.5 %copy-start.2 = (f32[2000]{0:T(1024)S(1)}, f32[2000]{0:T(1024)}, u32[]{:S(2)}) copy-start(f32[2000]{0:T(1024)} %param.8) | copy-start | bytes 24004
  132.6 54.3 %reduce-scatter.5.cloned.1.call-start = ((), (), s32[]{:S(2)}) async-start(), calls=%async_computation.6 | async-start | bytes 196608 | tf_op jit(solution)/shard_map/reduce_scatter | solution.py:46
  225.5 42.0 %copy-start.1 = (bf16[16,1500,32]{1,2,0:T(8,128)(2,1)S(1)}, bf16[16,1500,32]{1,2,0:T(8,128)(2,1)}, u32[]{:S(2)}) copy-start(bf16[16,1500,32]{1,2,0:T(8,128)(2,1)} %copy-done) | copy-start | bytes 4608004
Sparse Core Ops, SparseCore 0:
  34.2 48.1 all-gather.2
  132.7 36.9 reduce-scatter.2
  172.1 14.6 reduce-scatter.4
where the time goes:
time: 289 us; the launch traced here: 288 us
  waiting for transfers between devices  120 us (42%)
  blocking collectives  72.1 us (25%)
  local copies, waits for them, and re-layouts  38.9 us (13%)
  starting transfers between devices  27.4 us (9%)
  between operations  13.2 us (5%)
  matrix products  12.2 us (4%)
  other arithmetic  4.5 us (2%)
    reduce_scatter x2, waiting for transfers between devices, reduced_to_own(): pieces = lax.psum_scatter(pieces, axes[k], scatter_dimension=0, tiled=True)  52.5 us
    all_to_all x1, blocking collectives, sent_to_all(): return lax.all_to_all(copies, axis, split_axis=0, concat_axis=0, tiled=True)  41.8 us
    all_to_all x1, waiting for transfers between devices, sent_to_all(): return lax.all_to_all(copies, axis, split_axis=0, concat_axis=0, tiled=True)  35.1 us
    all_gather x2, blocking collectives, stacked_from(): pieces = lax.all_gather(pieces, axes[k], axis=0, tiled=True)  30.3 us
    all_to_all x1, waiting for transfers between devices, summed_on_arrival(): lax.all_to_all(cut_along(shard, dim, count), axis, 0, 0, tiled=True)  28.9 us
    all_to_all x1, starting transfers between devices, sent_to_all(): return lax.all_to_all(copies, axis, split_axis=0, concat_axis=0, tiled=True)  22.8 us
    convert_element_type x1, local copies, waits for them, and re-layouts, per_device(): return total.astype(jnp.bfloat16)  9.19 us
    unnamed x7, local copies, waits for them, and re-layouts  6.63 us
  transfers between devices with their start and end apart: 5, of which 5 were waited for; matrix products, arithmetic and copies ran while one was open for 6% of the time, Pallas kernels for 0%

commit v1 on v0

--- a/solution.py
+++ b/solution.py
@@ -50,7 +50,9 @@
 def stacked_from(shard, axes, order):
     pieces = shard[None]
     for k in order:
-        pieces = lax.all_gather(pieces, axes[k], axis=0, tiled=True)
+        pieces = jnp.concatenate(
+            lax.all_to_all(jnp.stack([pieces] * lax.axis_size(axes[k])), axes[k], 0, 0), axis=0
+        )
     carried = [lax.axis_size(axes[k]) for k in reversed(order)]
     pieces = pieces.reshape(*carried, *shard.shape)
     turned = sorted(range(len(order)), key=lambda place: order[len(order) - 1 - place])

time: 289 us -> 310 us (1.073); the launches traced: 288 us -> 304 us
  waiting for transfers between devices: 120 us -> 146 us
  blocking collectives: 72.1 us -> 47.6 us
  starting transfers between devices: 27.4 us -> 34.7 us
  local copies, waits for them, and re-layouts: 38.9 us -> 43.1 us
    all_gather x2 -> x0, blocking collectives: 30.3 us -> none  [stacked_from(): pieces = lax.all_gather(pieces, axes[k], axis=0, tiled=True)]
    all_to_all x0 -> x1, waiting for transfers between devices: none -> 24.9 us  [stacked_from(): lax.all_to_all(jnp.stack([pieces] * lax.axis_size(axes[k])), axes[k], 0, 0)]
    all_to_all x0 -> x1, starting transfers between devices: none -> 7.26 us  [stacked_from(): lax.all_to_all(jnp.stack([pieces] * lax.axis_size(axes[k])), axes[k], 0, 0)]
    all_to_all x0 -> x1, blocking collectives: none -> 3.85 us  [stacked_from(): lax.all_to_all(jnp.stack([pieces] * lax.axis_size(axes[k])), axes[k], 0, 0)]
  transfers between devices with their start and end apart: 5 -> 6, of which waited for: 5 -> 6; matrix products, arithmetic and copies ran while one was open for 6% -> 7% of each run, Pallas kernels for 0% -> 0%
where the time goes in v1:
time: 310 us; the launch traced here: 304 us
  waiting for transfers between devices  146 us (47%)
  blocking collectives  47.6 us (15%)
  local copies, waits for them, and re-layouts  43.1 us (14%)
  starting transfers between devices  34.7 us (11%)
  matrix products  13.3 us (4%)
  between operations  13.2 us (4%)
  other arithmetic  5.43 us (2%)
    reduce_scatter x2, waiting for transfers between devices, reduced_to_own(): pieces = lax.psum_scatter(pieces, axes[k], scatter_dimension=0, tiled=True)  54.2 us
    all_to_all x1, blocking collectives, sent_to_all(): return lax.all_to_all(copies, axis, split_axis=0, concat_axis=0, tiled=True)  43.8 us
    all_to_all x1, waiting for transfers between devices, sent_to_all(): return lax.all_to_all(copies, axis, split_axis=0, concat_axis=0, tiled=True)  35.1 us
    all_to_all x1, waiting for transfers between devices, summed_on_arrival(): lax.all_to_all(cut_along(shard, dim, count), axis, 0, 0, tiled=True)  31.1 us
    all_to_all x1, waiting for transfers between devices, stacked_from(): lax.all_to_all(jnp.stack([pieces] * lax.axis_size(axes[k])), axes[k], 0, 0)  24.9 us
    all_to_all x1, starting transfers between devices, sent_to_all(): return lax.all_to_all(copies, axis, split_axis=0, concat_axis=0, tiled=True)  22.8 us
    convert_element_type x1, local copies, waits for them, and re-layouts, per_device(): return total.astype(jnp.bfloat16)  9.19 us
    all_to_all x1, starting transfers between devices, stacked_from(): lax.all_to_all(jnp.stack([pieces] * lax.axis_size(axes[k])), axes[k], 0, 0)  7.26 us
  transfers between devices with their start and end apart: 6, of which 6 were waited for; matrix products, arithmetic and copies ran while one was open for 7% of the time, Pallas kernels for 0%

profile of v1, /device:TPU:516, one launch (start us, length us, event | category | flops | bytes accessed | tf_op | source)
XLA Modules:
  0.0 303.6 jit_solution(12539879394825256082)
XLA Ops:
  6.5 2.2 broadcast_in_dim.4
  8.7 22.8 %all-to-all-start = ((bf16[16,1500,32]{1,2,0:T(8,128)(2,1)}), bf16[16,1500,32]{1,2,0:T(8,128)(2,1)S(1)}, u32[]{:S(2)}, u32[]{:S(2)}) async-start(bf16[16,1500,32]{1,2,0:T(8,128)(2,1)} %broadcast_in_dim.4), calls=%async_computation | async-start | bytes 3145728 | tf_op jit(solution)/shard_map/all_to_all | solution.py:18
  31.5 0.1 all-gather.3.cloned.1.call-start
  31.6 0.7 all-gather.3.cloned.1.call-update
  32.3 35.1 %all-to-all-done = bf16[16,1500,32]{1,2,0:T(8,128)(2,1)S(1)} async-done(((bf16[16,1500,32]{1,2,0:T(8,128)(2,1)}), bf16[16,1500,32]{1,2,0:T(8,128)(2,1)S(1)}, u32[]{:S(2)}, u32[]{:S(2)}) %all-to-all-start) | async-done | bytes 1536032 | tf_op jit(solution)/shard_map/all_to_all | solution.py:18
  67.4 0.0 copy-start
  67.4 1.2 copy-done
  68.6 6.1 %fusion.9 = bf16[512,2,750]{0,2,1:T(8,128)(2,1)} fusion(bf16[1500,512,1]{0,1,2:T(8,128)(2,1)S(1)} %bitcast.42, bf16[2,750,1500]{2,0,1:T(2,128)(2,1)} %param.5), kind=kOutput, calls=%fused_computation.9 | convolution fusion | flops 2304768000 | bytes 7572000 | tf_op jit(solution)/shard_map/pij,jv->vpi/dot_general | solution.py:75
  74.7 1.7 copy.24
  76.4 1.3 copy.25
  77.7 4.5 %all-to-all-start.1 = ((bf16[8,64,2,750]{3,1,2,0:T(8,128)(2,1)}), bf16[8,64,2,750]{3,1,2,0:T(8,128)(2,1)}, u32[]{:S(2)}, u32[]{:S(2)}) async-start(bf16[8,64,2,750]{3,1,2,0:T(8,128)(2,1)} %copy.25), calls=%async_computation.1 | async-start | bytes 3145728 | tf_op jit(solution)/shard_map/all_to_all | solution.py:32
  82.2 0.1 reduce-scatter.3.cloned.1.call-start
  82.2 0.1 all-gather.3.cloned.1.call-done
  82.3 4.6 %copy.26 = bf16[8,250,750]{1,0,2:T(8,128)(2,1)} copy(bf16[8,250,750]{1,2,0:T(8,128)(2,1)} %all-gather.3.cloned.1.call-done) | data formatting | bytes 6000000 | tf_op jit(solution)/shard_map/all_gather | solution.py:71
  86.9 5.5 %reshape.44 = bf16[2000,750]{0,1:T(8,128)(2,1)S(1)} reshape(bf16[8,250,750]{1,0,2:T(8,128)(2,1)} %copy.26) | data formatting | bytes 6000000
  92.4 31.1 %all-to-all-done.1 = bf16[8,64,2,750]{3,1,2,0:T(8,128)(2,1)} async-done(((bf16[8,64,2,750]{3,1,2,0:T(8,128)(2,1)}), bf16[8,64,2,750]{3,1,2,0:T(8,128)(2,1)}, u32[]{:S(2)}, u32[]{:S(2)}) %all-to-all-start.1) | async-done | bytes 1536032 | tf_op jit(solution)/shard_map/all_to_all | solution.py:32
  123.5 1.7 convert_reduce_fusion
  125.2 1.5 fusion.6
  126.6 1.8 copy.28
  128.4 3.5 %reshape_reshape_reshape.3 = f32[16,250,64]{1,0,2:T(8,128)} reshape(f32[2,2000,64]{1,0,2:T(2,128)} %copy.28) | data formatting | bytes 2048000 | tf_op jit(solution)/shard_map/reshape;reshape;reshape | solution.py:44
  131.9 2.8 copy.29
  134.7 0.0 copy-start.2
  134.7 0.1 reduce-scatter.3.cloned.1.call-update
  134.7 0.1 reduce-scatter.5.cloned.1.call-start
  134.8 37.0 %reduce-scatter.3.cloned.1.call-done = f32[2,250,64]{1,2,0:T(8,128)} async-done(((f32[16,250,64]{1,2,0:T(8,128)}), f32[2,250,64]{1,2,0:T(8,128)}) %reduce-scatter.3.cloned.1.call-update) | async-done | bytes 128016 | tf_op jit(solution)/shard_map/reduce_scatter | solution.py:46
  171.8 0.1 reduce-scatter.5.cloned.1.call-update
  171.9 17.1 %reduce-scatter.5.cloned.1.call-done = f32[1,250,64]{1,2,0:T(8,128)} async-done(((f32[2,250,64]{1,2,0:T(8,128)}), f32[1,250,64]{1,2,0:T(8,128)}) %reduce-scatter.5.cloned.1.call-update) | async-done | bytes 64016 | tf_op jit(solution)/shard_map/reduce_scatter | solution.py:46
  189.0 0.9 pad_maximum_fusion
  190.0 3.9 %all_to_all.25 = f32[2,1,250,64]{2,3,1,0:T(8,128)S(1)} all-to-all(f32[2,1,250,64]{2,3,1,0:T(8,128)S(1)} %pad_maximum_fusion), channel_id=1, replica_groups=mesh['grp'=2,'row_0'=8,'row_1'=2,'col'=8] {'row_1'}, dimensions={0} | all-to-all | bytes 256000 | tf_op jit(solution)/shard_map/all_to_all | solution.py:54
  193.8 0.1 copy.30
  193.9 1.2 stack.7
  195.2 7.3 %all-to-all-start.3 = ((f32[8,2,250,64]{2,1,3,0:T(2,128)}), f32[8,2,250,64]{2,1,3,0:T(2,128)}, u32[]{:S(2)}, u32[]{:S(2)}) async-start(f32[8,2,250,64]{2,1,3,0:T(2,128)} %stack.7), calls=%async_computation.5 | async-start | bytes 2097152 | tf_op jit(solution)/shard_map/all_to_all | solution.py:54
  202.4 0.8 dynamic_slice.3
  203.2 0.0 copy-done.2
  203.2 0.9 broadcast_subtract_fusion
  204.1 24.9 %all-to-all-done.3 = f32[8,2,250,64]{2,1,3,0:T(2,128)} async-done(((f32[8,2,250,64]{2,1,3,0:T(2,128)}), f32[8,2,250,64]{2,1,3,0:T(2,128)}, u32[]{:S(2)}, u32[]{:S(2)}) %all-to-all-start.3) | async-done | bytes 1024032 | tf_op jit(solution)/shard_map/all_to_all | solution.py:54
  228.9 2.8 copy.31
  231.7 4.3 %reshape_reshape_reshape_reshape_reshape.3 = f32[2,2000,64]{1,0,2:T(2,128)} reshape(f32[8,2,250,64]{2,1,0,3:T(2,128)} %copy.31) | data formatting | bytes 2048000 | tf_op jit(solution)/shard_map/reshape;reshape;reshape;reshape;reshape | solution.py:67
  236.1 1.9 divide_convert_fusion
  238.0 1.1 fusion.15
  239.1 0.1 broadcast_in_dim.10
  239.2 0.0 copy-start.1
  239.2 43.8 %all_to_all.26 = bf16[8,2,750,64]{2,3,1,0:T(8,128)(2,1)S(1)} all-to-all(bf16[8,2,750,64]{2,3,1,0:T(8,128)(2,1)S(1)} %broadcast_in_dim.10), channel_id=1, replica_groups=mesh['grp'=2,'row_0'=8,'row_1'=2,'col'=8] {'col'}, dimensions={0} | all-to-all | bytes 3072000 | tf_op jit(solution)/shard_map/all_to_all | solution.py:18
  283.0 0.1 copy.34
  283.1 0.0 copy-done.1
  283.1 4.7 %convolution_convert_fusion = bf16[2,750,1500]{2,1,0:T(8,128)(2,1)} fusion(bf16[2,750,512]{1,2,0:T(8,128)(2,1)S(1)} %bitcast.44, bf16[1500,512,1]{0,1,2:T(8,128)(2,1)S(1)} %bitcast.43), kind=kOutput, calls=%fused_computation.2 | convolution fusion | flops 2306249984 | bytes 7572000 | tf_op jit(solution)/shard_map/piv,jv->pij/dot_general | solution.py:92
  287.8 9.2 %copy.37 = bf16[2,750,1500]{2,0,1:T(2,128)(2,1)} copy(bf16[2,750,1500]{2,1,0:T(8,128)(2,1)} %convolution_convert_fusion) | data formatting | bytes 9000000 | tf_op jit(solution)/shard_map/convert_element_type | solution.py:95
Async XLA Ops:
  8.7 58.7 %all-to-all-start = ((bf16[16,1500,32]{1,2,0:T(8,128)(2,1)}), bf16[16,1500,32]{1,2,0:T(8,128)(2,1)S(1)}, u32[]{:S(2)}, u32[]{:S(2)}) async-start(bf16[16,1500,32]{1,2,0:T(8,128)(2,1)} %broadcast_in_dim.4), calls=%async_computation | async-start | bytes 3145728 | tf_op jit(solution)/shard_map/all_to_all | solution.py:18
  31.5 50.8 %all-gather.3.cloned.1.call-start = ((), (), s32[]{:S(2)}) async-start(), calls=%async_computation.9 | async-start | bytes 3465216 | tf_op jit(solution)/shard_map/all_gather | solution.py:71
  67.4 1.2 copy-start
  77.7 45.8 %all-to-all-start.1 = ((bf16[8,64,2,750]{3,1,2,0:T(8,128)(2,1)}), bf16[8,64,2,750]{3,1,2,0:T(8,128)(2,1)}, u32[]{:S(2)}, u32[]{:S(2)}) async-start(bf16[8,64,2,750]{3,1,2,0:T(8,128)(2,1)} %copy.25), calls=%async_computation.1 | async-start | bytes 3145728 | tf_op jit(solution)/shard_map/all_to_all | solution.py:32
  82.2 89.7 %reduce-scatter.3.cloned.1.call-start = ((), (), s32[]{:S(2)}) async-start(), calls=%async_computation.7 | async-start | bytes 1179648 | tf_op jit(solution)/shard_map/reduce_scatter | solution.py:46
  134.7 68.5 %copy-start.2 = (f32[2000]{0:T(1024)S(1)}, f32[2000]{0:T(1024)}, u32[]{:S(2)}) copy-start(f32[2000]{0:T(1024)} %param.8) | copy-start | bytes 24004
  134.7 54.3 %reduce-scatter.5.cloned.1.call-start = ((), (), s32[]{:S(2)}) async-start(), calls=%async_computation.8 | async-start | bytes 196608 | tf_op jit(solution)/shard_map/reduce_scatter | solution.py:46
  195.2 33.8 %all-to-all-start.3 = ((f32[8,2,250,64]{2,1,3,0:T(2,128)}), f32[8,2,250,64]{2,1,3,0:T(2,128)}, u32[]{:S(2)}, u32[]{:S(2)}) async-start(f32[8,2,250,64]{2,1,3,0:T(2,128)} %stack.7), calls=%async_computation.5 | async-start | bytes 2097152 | tf_op jit(solution)/shard_map/all_to_all | solution.py:54
  239.2 43.9 %copy-start.1 = (bf16[16,1500,32]{1,2,0:T(8,128)(2,1)S(1)}, bf16[16,1500,32]{1,2,0:T(8,128)(2,1)}, u32[]{:S(2)}) copy-start(bf16[16,1500,32]{1,2,0:T(8,128)(2,1)} %copy-done) | copy-start | bytes 4608004
Sparse Core Ops, SparseCore 0:
  34.2 48.1 all-gather.2
  134.9 36.9 reduce-scatter.2
  174.3 14.6 reduce-scatter.4
